TPU v7x, 32 devices: a whole 2x2x4 slice. The times are simulated.
32 devices in a mesh: dp: 8 (over y, x, core), expert: 4 (over z).
Axes of the slice: x: 2, y: 2, z: 4, core: 2. Of those that a mesh axis runs over, the one named last changes fastest.
Arguments:
- tokens: bfloat16 [4096, 1792], P(('dp', 'expert')), may hold values from -6 to 6
- routes: int32 [4096, 2], P(('dp', 'expert')), may hold values from 0 to 3, all different within a row; in each aligned block of 128 rows (0 to 127, 128 to 255, ...) at most 128 rows name the same one
- gates: float32 [4096, 2], P(('dp', 'expert')), may hold values from 0.25 to 1
- grad_hidden: bfloat16 [4096, 2, 512], P(('dp', 'expert')), may hold values from -4 to 4
- w_in: bfloat16 [4, 1792, 512], P('expert', 'dp'), may hold values from -0.25 to 0.25
- error: bfloat16 [8, 4, 1792, 512], P('dp', 'expert'), may hold values from -6 to 6
- q_seed: float32 [4, 512, 32], P('expert'), may hold values from -6 to 6
Outputs:
- grad_tokens: bfloat16 [4096, 1792], P(('dp', 'expert'))
- error_next: bfloat16 [8, 4, 1792, 512], P('dp', 'expert')
- weight_grad: float32 [4, 1792, 512], P('expert', 'dp')
Inputs may be any that keep to these rules, and one draw needn't show every extreme that they name: `routes`: in the rows of one device no expert is named by more than 128 rows, a bound that some block reaches; the two experts of a row differ.
All inputs are finite; a program needn't handle non-finite values.
Results may differ from a plain program's by a relative error of at most 0.014.
Values may be sent and summed in bfloat16 or wider, within the bound.
A program may use at most 64 MiB of HBM per device.

v0:
```python
import jax
import jax.numpy as jnp
from jax import lax
from jax.sharding import PartitionSpec as P

highest = lax.Precision.HIGHEST


def slopes(pre_act):
    squashed = jax.nn.sigmoid(pre_act)
    return squashed * (1.0 + pre_act * (1.0 - squashed))


def body(tokens, routes, gates, grad_hidden, w_in, error, q_seed):
    experts = lax.axis_size("expert")
    replicas = lax.axis_size("dp")
    row_count = tokens.shape[0]
    width = tokens.shape[1]
    hidden = grad_hidden.shape[2]
    capacity = 4 * row_count // experts
    chosen = routes.reshape(-1)
    matches = (chosen[:, None] == jnp.arange(experts, dtype=jnp.int32)[None, :]).astype(jnp.int32)
    earlier = jnp.cumsum(matches, axis=0) - matches
    position = chosen * capacity + jnp.sum(earlier * matches, axis=1)
    placer = (jnp.arange(experts * capacity, dtype=jnp.int32)[:, None] == position[None, :]).astype(
        jnp.bfloat16
    )
    gate_flat = gates.reshape(-1)
    scaled = (jnp.repeat(tokens, 2, axis=0).astype(jnp.float32) * gate_flat[:, None]).astype(
        jnp.bfloat16
    )
    sent_rows = jnp.dot(placer, scaled, preferred_element_type=jnp.float32).astype(jnp.bfloat16)
    sent_grad = jnp.dot(
        placer, grad_hidden.reshape(2 * row_count, hidden), preferred_element_type=jnp.float32
    ).astype(jnp.bfloat16)
    sent_rows = sent_rows.reshape(experts, capacity, width)
    sent_grad = sent_grad.reshape(experts, capacity, hidden)
    weight_part = w_in[0]
    arrived, arrived_grad = (
        lax.all_to_all(sent_rows, "expert", split_axis=0, concat_axis=0, tiled=True),
        lax.all_to_all(sent_grad, "expert", split_axis=0, concat_axis=0, tiled=True),
    )
    arrived = arrived.reshape(experts * capacity, width)
    arrived_grad = arrived_grad.reshape(experts * capacity, hidden)
    pre_act = jnp.dot(
        arrived,
        lax.all_gather(weight_part, "dp", axis=0, tiled=True),
        preferred_element_type=jnp.float32,
    )
    grad_pre = (arrived_grad.astype(jnp.float32) * slopes(pre_act)).astype(jnp.bfloat16)
    weight_term = lax.dot_general(
        arrived, grad_pre, (((0,), (0,)), ((), ())), preferred_element_type=jnp.float32
    )
    grad_rows = lax.dot_general(
        grad_pre,
        lax.all_gather(weight_part, "dp", axis=0, tiled=True),
        (((1,), (1,)), ((), ())),
        preferred_element_type=jnp.float32,
    )
    sending = grad_rows.astype(jnp.bfloat16).reshape(experts, capacity, width)
    returned = lax.all_to_all(sending, "expert", split_axis=0, concat_axis=0, tiled=True).reshape(
        experts * capacity, width
    )
    picked = jnp.take(returned, position, axis=0).astype(jnp.float32) * gate_flat[:, None]
    grad_tokens = jnp.sum(picked.reshape(row_count, 2, width), axis=1).astype(jnp.bfloat16)
    merged = weight_term + error[0, 0].astype(jnp.float32)
    q_start = q_seed[0]
    local_factor = lax.dot_general(q_start, merged, (((0,), (1,)), ((), ())), precision=highest)
    part_rows = lax.psum_scatter(local_factor, "dp", scatter_dimension=1, tiled=True) / replicas
    gram_matrix = lax.psum(jnp.dot(part_rows, part_rows.T, precision=highest), "dp")
    lower_factor = jnp.linalg.cholesky(gram_matrix)
    part_basis = jax.scipy.linalg.solve_triangular(lower_factor, part_rows, lower=True)
    basis = lax.all_gather(part_basis, "dp", axis=1, tiled=True)
    q_factor = (
        lax.psum(jnp.dot(basis, merged, precision=highest).astype(jnp.bfloat16), "dp").astype(
            jnp.float32
        )
        / replicas
    )
    low_rank = lax.dot_general(basis, q_factor, (((0,), (0,)), ((), ())), precision=highest)
    error_next = (merged - low_rank).astype(jnp.bfloat16)[None, None]
    shard_rows = width // replicas
    weight_grad = lax.dynamic_slice_in_dim(
        low_rank, lax.axis_index("dp") * shard_rows, shard_rows, 0
    )[None]
    return (grad_tokens, error_next, weight_grad)


def solution(mesh):
    placed = (
        P(("dp", "expert"), None),
        P(("dp", "expert"), None),
        P(("dp", "expert"), None),
        P(("dp", "expert"), None, None),
        P("expert", "dp", None),
        P("dp", "expert", None, None),
        P("expert", None, None),
    )
    return jax.shard_map(
        body,
        mesh=mesh,
        in_specs=placed,
        out_specs=(
            P(("dp", "expert"), None),
            P("dp", "expert", None, None),
            P("expert", "dp", None),
        ),
        check_vma=False,
    )
```

profile of v0, /device:TPU:0, one launch (start us, length us, event | category | flops | bytes accessed | tf_op | source)
XLA Modules:
  0.0 212.3 jit_solution(1840900786812910726)
XLA Ops:
  12.1 6.3 %all-to-all-start = ((bf16[4,128,512]{2,1,0:T(8,128)(2,1)}), bf16[4,128,512]{2,1,0:T(8,128)(2,1)S(1)}, u32[]{:S(2)}, u32[]{:S(2)}) async-start(bf16[4,128,512]{2,1,0:T(8,128)(2,1)} %bitcast.2), calls=%async_computation | async-start | bytes 1048576 | tf_op jit(solution)/shard_map/all_to_all | solution.py:41
  19.2 1.7 broadcast_in_dim.25
  20.9 2.6 %convert_element_type.64 = f32[256,1792]{1,0:T(8,128)S(1)} reshape(f32[128,2,1792]{2,1,0:T(2,128)} %broadcast_in_dim.25) | data formatting | bytes 3670016 | tf_op jit(solution)/shard_map/convert_element_type | solution.py:29
  23.8 2.0 convolution_convert_fusion
  25.7 7.3 %all-to-all-done = bf16[4,128,512]{2,1,0:T(8,128)(2,1)S(1)} async-done(((bf16[4,128,512]{2,1,0:T(8,128)(2,1)}), bf16[4,128,512]{2,1,0:T(8,128)(2,1)S(1)}, u32[]{:S(2)}, u32[]{:S(2)}) %all-to-all-start) | async-done | bytes 524320 | tf_op jit(solution)/shard_map/all_to_all | solution.py:41
  33.0 3.7 %all-to-all-start.1 = ((bf16[4,128,1792]{2,1,0:T(8,128)(2,1)}), bf16[4,128,1792]{2,1,0:T(8,128)(2,1)S(1)}, u32[]{:S(2)}, u32[]{:S(2)}) async-start(bf16[4,128,1792]{2,1,0:T(8,128)(2,1)} %bitcast.74), calls=%async_computation.1 | async-start | bytes 3670016 | tf_op jit(solution)/shard_map/all_to_all | solution.py:40
  37.2 41.6 %all-to-all-done.1 = bf16[4,128,1792]{2,1,0:T(8,128)(2,1)S(1)} async-done(((bf16[4,128,1792]{2,1,0:T(8,128)(2,1)}), bf16[4,128,1792]{2,1,0:T(8,128)(2,1)S(1)}, u32[]{:S(2)}, u32[]{:S(2)}) %all-to-all-start.1) | async-done | bytes 1835040 | tf_op jit(solution)/shard_map/all_to_all | solution.py:40
  78.8 3.0 %fusion.4 = bf16[512,512]{1,0:T(8,128)(2,1)S(1)} fusion(bf16[512,512]{1,0:T(8,128)(2,1)S(1)} %bitcast.77, bf16[512,1792]{1,0:T(8,128)(2,1)S(1)} %bitcast.72, bf16[1,1792,512]{2,1,0:T(8,128)(2,1)} %all-gather.4.cloned.1.call-done), kind=kOutput, calls=%fused_computation.17 | convolution fusion | flops 942145536 | bytes 4718592 | tf_op jit(solution)/shard_map/dot_general | solution.py:45
  83.0 1.8 copy-done.1
  84.8 3.4 %convolution_bitcast_fusion = f32[32,1792]{1,0:T(8,128)S(1)} fusion(f32[1792,512]{1,0:T(8,128)S(1)} %convert_add_fusion, f32[1,512,32]{1,2,0:T(8,128)S(1)} %copy-done), kind=kOutput, calls=%fused_computation.5 | convolution fusion | flops 352321536 | bytes 3964928 | tf_op jit(solution)/shard_map/dot_general | solution.py:68
  88.2 1.2 copy.49
  89.5 3.9 %convolution_convert_fusion.1 = bf16[512,1792]{1,0:T(8,128)(2,1)} fusion(bf16[512,512]{1,0:T(8,128)(2,1)S(1)} %fusion.4, bf16[1,1792,512]{2,1,0:T(8,128)(2,1)} %all-gather.4.cloned.1.call-done), kind=kOutput, calls=%fused_computation.4 | convolution fusion | flops 940441600 | bytes 4194304 | tf_op jit(solution)/shard_map/dot_general | solution.py:54
  93.4 3.6 %all-to-all-start.2 = ((bf16[4,128,1792]{2,1,0:T(8,128)(2,1)}), bf16[4,128,1792]{2,1,0:T(8,128)(2,1)S(1)}, u32[]{:S(2)}, u32[]{:S(2)}) async-start(bf16[4,128,1792]{2,1,0:T(8,128)(2,1)} %bitcast.76), calls=%async_computation.2 | async-start | bytes 3670016 | tf_op jit(solution)/shard_map/all_to_all | solution.py:61
  97.2 27.0 %reduce-scatter.4.cloned.1.call-done = f32[224,32]{1,0:T(8,128)} async-done(((f32[1792,32]{1,0:T(8,128)}), f32[224,32]{1,0:T(8,128)}) %reduce-scatter.4.cloned.1.call-update) | async-done | bytes 28688
  125.3 23.2 %psum.14 = f32[32,32]{0,1:T(8,128)S(1)} all-reduce(f32[32,32]{0,1:T(8,128)S(1)} %fusion.16), channel_id=1, replica_groups=mesh['dp'=8,'expert'=4] {'dp'}, use_global_device_ids=true, to_apply=%region_5.6 | all-reduce | flops 1024 | bytes 8192 | tf_op jit(solution)/shard_map/psum | solution.py:70
  148.6 2.9 %cholesky.16 = f32[32,32]{1,0:T(8,128)S(1)} custom-call(f32[32,32]{1,0:T(8,128)S(1)} %fusion.20), custom_call_target="Cholesky" | custom-call | tf_op jit(solution)/shard_map/jit(cholesky)/cholesky | solution.py:71
  152.9 2.4 %custom-call.7 = f32[1,32,32]{1,2,0:T(8,128)S(1)} custom-call(f32[1,32,32]{2,1,0:T(8,128)S(1)} %fusion.18), custom_call_target="InvertDiagBlocksLowerTriangular" | custom-call | tf_op jit(solution)/shard_map/jit(_solve_triangular)/triangular_solve | solution.py:72
  155.6 9.6 %all-gather.1 = f32[8,224,32]{1,2,0:T(8,128)S(1)} all-gather(f32[1,224,32]{1,2,0:T(8,128)S(1)} %convolution_bitcast_fusion.1), channel_id=1, replica_groups=mesh['dp'=8,'expert'=4] {'dp'}, dimensions={0}, use_global_device_ids=true | all-gather | bytes 258048 | tf_op jit(solution)/shard_map/all_gather | solution.py:73
  165.5 4.2 %convolution_convert_fusion.3 = bf16[32,512]{1,0:T(8,128)(2,1)S(1)} fusion(f32[1792,32]{0,1:T(8,128)S(1)} %reshape.137, f32[1792,512]{1,0:T(8,128)} %copy-done.1), kind=kOutput, calls=%fused_computation.14 | convolution fusion | flops 352337920 | bytes 3932160 | tf_op jit(solution)/shard_map/dot_general | solution.py:75
  169.7 23.6 %psum.15 = bf16[32,512]{1,0:T(8,128)(2,1)S(1)} all-reduce(bf16[32,512]{1,0:T(8,128)(2,1)S(1)} %convolution_convert_fusion.3), channel_id=1, replica_groups=mesh['dp'=8,'expert'=4] {'dp'}, use_global_device_ids=true, to_apply=%region_8.9 | all-reduce | flops 16384 | bytes 65536 | tf_op jit(solution)/shard_map/psum | solution.py:75
  193.3 3.1 %fusion.11 = f32[1792,512]{1,0:T(8,128)S(1)} fusion(f32[1792,32]{0,1:T(8,128)S(1)} %reshape.137, bf16[32,512]{1,0:T(8,128)(2,1)S(1)} %psum.15), kind=kOutput, calls=%fused_computation.24 | convolution fusion | flops 352354304 | bytes 3932160 | tf_op jit(solution)/shard_map/dot_general | solution.py:80
  197.2 2.0 fusion
  199.2 1.3 gather_fusion
  200.9 4.5 %multiply_reduce_fusion = bf16[128,1792]{1,0:T(8,128)(2,1)} fusion(bf16[128,2,1792]{2,1,0:T(2,128)(2,1)S(1)} %gather.7, pred[128,2]{1,0:T(8,128)(4,1)S(1)} %copy.41, f32[128,2]{1,0:T(8,128)S(1)} %copy.42), kind=kLoop, calls=%fused_computation.10 | loop fusion | flops 1605632 | bytes 1377536 | tf_op jit(solution)/shard_map/reduce_sum | solution.py:65
  (58 shorter events, 12.0 us)
Async XLA Ops:
  7.2 77.6 %copy-start = (f32[1,512,32]{1,2,0:T(8,128)S(1)}, f32[1,512,32]{1,2,0:T(8,128)}, u32[]{:S(2)}) copy-start(f32[1,512,32]{1,2,0:T(8,128)} %param.13) | copy-start | bytes 196612
  7.2 12.0 %copy-start.4 = (bf16[128,1792]{1,0:T(8,128)(2,1)S(1)}, bf16[128,1792]{1,0:T(8,128)(2,1)}, u32[]{:S(2)}) copy-start(bf16[128,1792]{1,0:T(8,128)(2,1)} %param.7) | copy-start | bytes 1376260
  12.1 20.8 %all-to-all-start = ((bf16[4,128,512]{2,1,0:T(8,128)(2,1)}), bf16[4,128,512]{2,1,0:T(8,128)(2,1)S(1)}, u32[]{:S(2)}, u32[]{:S(2)}) async-start(bf16[4,128,512]{2,1,0:T(8,128)(2,1)} %bitcast.2), calls=%async_computation | async-start | bytes 1048576 | tf_op jit(solution)/shard_map/all_to_all | solution.py:41
  18.5 60.3 %all-gather.4.cloned.1.call-start = ((), (), s32[]{:S(2)}) async-start(), calls=%async_computation.4 | async-start | bytes 2064384 | tf_op jit(solution)/shard_map/all_gather | solution.py:47
  20.9 2.6 %copy-start.6 = (f32[128,2]{0,1:T(2,128)S(1)}, f32[128,2]{0,1:T(2,128)}, u32[]{:S(2)}) copy-start(f32[128,2]{0,1:T(2,128)} %param.9) | copy-start | bytes 3076
  33.0 3.9 %copy-start.5 = (s32[128,2]{0,1:T(2,128)S(1)}, s32[128,2]{0,1:T(2,128)}, u32[]{:S(2)}) copy-start(s32[128,2]{0,1:T(2,128)} %param.8) | copy-start | bytes 3076
  33.0 45.8 %all-to-all-start.1 = ((bf16[4,128,1792]{2,1,0:T(8,128)(2,1)}), bf16[4,128,1792]{2,1,0:T(8,128)(2,1)S(1)}, u32[]{:S(2)}, u32[]{:S(2)}) async-start(bf16[4,128,1792]{2,1,0:T(8,128)(2,1)} %bitcast.74), calls=%async_computation.1 | async-start | bytes 3670016 | tf_op jit(solution)/shard_map/all_to_all | solution.py:40
  36.7 87.5 %reduce-scatter.4.cloned.1.call-start = ((), (), s32[]{:S(2)}) async-start(), calls=%async_computation.5 | async-start | bytes 1032192
  78.8 3.0 %copy-start.3 = (bf16[1,1,1792,512]{3,2,1,0:T(8,128)(2,1)S(1)}, bf16[1,1,1792,512]{3,2,1,0:T(8,128)(2,1)}, u32[]{:S(2)}) copy-start(bf16[1,1,1792,512]{3,2,1,0:T(8,128)(2,1)} %param.12) | copy-start | bytes 5505028
  83.0 1.8 copy-start.1
  93.4 105.8 %all-to-all-start.2 = ((bf16[4,128,1792]{2,1,0:T(8,128)(2,1)}), bf16[4,128,1792]{2,1,0:T(8,128)(2,1)S(1)}, u32[]{:S(2)}, u32[]{:S(2)}) async-start(bf16[4,128,1792]{2,1,0:T(8,128)(2,1)} %bitcast.76), calls=%async_computation.2 | async-start | bytes 3670016 | tf_op jit(solution)/shard_map/all_to_all | solution.py:61
  193.3 3.9 %copy-start.2 = (f32[1792,512]{1,0:T(8,128)S(1)}, f32[1792,512]{1,0:T(8,128)}, u32[]{:S(2)}) copy-start(f32[1792,512]{1,0:T(8,128)} %copy-done.1) | copy-start | bytes 11010052
Sparse Core Ops, SparseCore 0:
  21.2 28.1 all-gather.3
  89.6 34.5 reduce-scatter.3
where the time goes:
time: 213 us; the launch traced here: 212 us
  waiting for transfers between devices  76.5 us (36%)
  blocking collectives  56.4 us (26%)
  matrix products  22.3 us (10%)
  other arithmetic  14.6 us (7%)
  local copies, waits for them, and re-layouts  14.4 us (7%)
  between operations  14.3 us (7%)
  starting transfers between devices  13.7 us (6%)
    all_to_all x1, waiting for transfers between devices, body(): lax.all_to_all(sent_rows, 'expert', split_axis=0, concat_axis=0, tiled=True)  41.6 us
    unnamed x3, waiting for transfers between devices  27.7 us
    psum x1, blocking collectives, body(): lax.psum(jnp.dot(basis, merged, precision=highest).astype(jnp.bfloat16),...  23.6 us
    psum x1, blocking collectives, body(): lax.psum(jnp.dot(part_rows, part_rows.T, precision=highest), 'dp')  23.2 us
    all_gather x1, blocking collectives, body(): basis = lax.all_gather(part_basis, 'dp', axis=1, tiled=True)  9.58 us
    all_to_all x1, waiting for transfers between devices, body(): lax.all_to_all(sent_grad, 'expert', split_axis=0, concat_axis=0, tiled=True)  7.26 us
    all_to_all x1, starting transfers between devices, body(): lax.all_to_all(sent_grad, 'expert', split_axis=0, concat_axis=0, tiled=True)  6.34 us
    unnamed x19, local copies, waits for them, and re-layouts  5.1 us
  transfers between devices with their start and end apart: 5, of which 3 were waited for; matrix products, arithmetic and copies ran while one was open for 14% of the time, Pallas kernels for 0%

commit v1 on v0

--- a/solution.py
+++ b/solution.py
@@ -67,7 +67,9 @@
     q_start = q_seed[0]
     local_factor = lax.dot_general(q_start, merged, (((0,), (1,)), ((), ())), precision=highest)
     part_rows = lax.psum_scatter(local_factor, "dp", scatter_dimension=1, tiled=True) / replicas
-    gram_matrix = lax.psum(jnp.dot(part_rows, part_rows.T, precision=highest), "dp")
+    gram_matrix = jnp.sum(
+        lax.all_gather(jnp.dot(part_rows, part_rows.T, precision=highest), "dp"), axis=0
+    )
     lower_factor = jnp.linalg.cholesky(gram_matrix)
     part_basis = jax.scipy.linalg.solve_triangular(lower_factor, part_rows, lower=True)
     basis = lax.all_gather(part_basis, "dp", axis=1, tiled=True)

time: 213 us -> 198 us (0.930)
  blocking collectives: 56.4 us -> 41.3 us
    psum x1 -> x0, blocking collectives: 23.2 us -> none  [body(): lax.psum(jnp.dot(part_rows, part_rows.T, precision=highest), 'dp')]
    all_gather x0 -> x1, blocking collectives: none -> 9.17 us  [body(): lax.all_gather(jnp.dot(part_rows, part_rows.T, precision=highest), 'dp')]
  transfers between devices with their start and end apart: 5 -> 5, of which waited for: 3 -> 3; matrix products, arithmetic and copies ran while one was open for 14% -> 15% of each run, Pallas kernels for 0% -> 0%
where the time goes in v1:
time: 198 us; the launch traced here: 197 us
  waiting for transfers between devices  76.5 us (39%)
  blocking collectives  41.3 us (21%)
  matrix products  22.3 us (11%)
  other arithmetic  14.6 us (7%)
  local copies, waits for them, and re-layouts  14.4 us (7%)
  between operations  14.3 us (7%)
  starting transfers between devices  13.7 us (7%)
    all_to_all x1, waiting for transfers between devices, body(): lax.all_to_all(sent_rows, 'expert', split_axis=0, concat_axis=0, tiled=True)  41.6 us
    unnamed x3, waiting for transfers between devices  27.7 us
    psum x1, blocking collectives, body(): lax.psum(jnp.dot(basis, merged, precision=highest).astype(jnp.bfloat16),...  23.6 us
    all_gather x1, blocking collectives, body(): lax.all_gather(jnp.dot(part_rows, part_rows.T, precision=highest), 'dp')  9.17 us
    all_gather x1, blocking collectives, body(): basis = lax.all_gather(part_basis, 'dp', axis=1, tiled=True)  8.53 us
    all_to_all x1, waiting for transfers between devices, body(): lax.all_to_all(sent_grad, 'expert', split_axis=0, concat_axis=0, tiled=True)  7.26 us
    all_to_all x1, starting transfers between devices, body(): lax.all_to_all(sent_grad, 'expert', split_axis=0, concat_axis=0, tiled=True)  6.34 us
    unnamed x19, local copies, waits for them, and re-layouts  5.1 us
  transfers between devices with their start and end apart: 5, of which 3 were waited for; matrix products, arithmetic and copies ran while one was open for 15% of the time, Pallas kernels for 0%

profile of v1, /device:TPU:0, one launch (start us, length us, event | category | flops | bytes accessed | tf_op | source)
XLA Modules:
  0.0 197.2 jit_solution(2070369616936165324)
XLA Ops:
  12.1 6.3 %all-to-all-start = ((bf16[4,128,512]{2,1,0:T(8,128)(2,1)}), bf16[4,128,512]{2,1,0:T(8,128)(2,1)S(1)}, u32[]{:S(2)}, u32[]{:S(2)}) async-start(bf16[4,128,512]{2,1,0:T(8,128)(2,1)} %bitcast.2), calls=%async_computation | async-start | bytes 1048576 | tf_op jit(solution)/shard_map/all_to_all | solution.py:41
  19.2 1.7 broadcast_in_dim.25
  20.9 2.6 %convert_element_type.64 = f32[256,1792]{1,0:T(8,128)S(1)} reshape(f32[128,2,1792]{2,1,0:T(2,128)} %broadcast_in_dim.25) | data formatting | bytes 3670016 | tf_op jit(solution)/shard_map/convert_element_type | solution.py:29
  23.8 2.0 convolution_convert_fusion
  25.7 7.3 %all-to-all-done = bf16[4,128,512]{2,1,0:T(8,128)(2,1)S(1)} async-done(((bf16[4,128,512]{2,1,0:T(8,128)(2,1)}), bf16[4,128,512]{2,1,0:T(8,128)(2,1)S(1)}, u32[]{:S(2)}, u32[]{:S(2)}) %all-to-all-start) | async-done | bytes 524320 | tf_op jit(solution)/shard_map/all_to_all | solution.py:41
  33.0 3.7 %all-to-all-start.1 = ((bf16[4,128,1792]{2,1,0:T(8,128)(2,1)}), bf16[4,128,1792]{2,1,0:T(8,128)(2,1)S(1)}, u32[]{:S(2)}, u32[]{:S(2)}) async-start(bf16[4,128,1792]{2,1,0:T(8,128)(2,1)} %bitcast.75), calls=%async_computation.1 | async-start | bytes 3670016 | tf_op jit(solution)/shard_map/all_to_all | solution.py:40
  37.2 41.6 %all-to-all-done.1 = bf16[4,128,1792]{2,1,0:T(8,128)(2,1)S(1)} async-done(((bf16[4,128,1792]{2,1,0:T(8,128)(2,1)}), bf16[4,128,1792]{2,1,0:T(8,128)(2,1)S(1)}, u32[]{:S(2)}, u32[]{:S(2)}) %all-to-all-start.1) | async-done | bytes 1835040 | tf_op jit(solution)/shard_map/all_to_all | solution.py:40
  78.8 3.0 %fusion.4 = bf16[512,512]{1,0:T(8,128)(2,1)S(1)} fusion(bf16[512,512]{1,0:T(8,128)(2,1)S(1)} %bitcast.79, bf16[512,1792]{1,0:T(8,128)(2,1)S(1)} %bitcast.73, bf16[1,1792,512]{2,1,0:T(8,128)(2,1)} %all-gather.5.cloned.1.call-done), kind=kOutput, calls=%fused_computation.17 | convolution fusion | flops 942145536 | bytes 4718592 | tf_op jit(solution)/shard_map/dot_general | solution.py:45
  83.0 1.8 copy-done.1
  84.8 3.4 %convolution_bitcast_fusion = f32[32,1792]{1,0:T(8,128)S(1)} fusion(f32[1792,512]{1,0:T(8,128)S(1)} %convert_add_fusion, f32[1,512,32]{1,2,0:T(8,128)S(1)} %copy-done), kind=kOutput, calls=%fused_computation.5 | convolution fusion | flops 352321536 | bytes 3964928 | tf_op jit(solution)/shard_map/dot_general | solution.py:68
  88.2 1.2 copy.44
  89.5 3.9 %convolution_convert_fusion.1 = bf16[512,1792]{1,0:T(8,128)(2,1)} fusion(bf16[512,512]{1,0:T(8,128)(2,1)S(1)} %fusion.4, bf16[1,1792,512]{2,1,0:T(8,128)(2,1)} %all-gather.5.cloned.1.call-done), kind=kOutput, calls=%fused_computation.4 | convolution fusion | flops 940441600 | bytes 4194304 | tf_op jit(solution)/shard_map/dot_general | solution.py:54
  93.4 3.6 %all-to-all-start.2 = ((bf16[4,128,1792]{2,1,0:T(8,128)(2,1)}), bf16[4,128,1792]{2,1,0:T(8,128)(2,1)S(1)}, u32[]{:S(2)}, u32[]{:S(2)}) async-start(bf16[4,128,1792]{2,1,0:T(8,128)(2,1)} %bitcast.77), calls=%async_computation.2 | async-start | bytes 3670016 | tf_op jit(solution)/shard_map/all_to_all | solution.py:61
  97.2 27.0 %reduce-scatter.4.cloned.1.call-done = f32[224,32]{1,0:T(8,128)} async-done(((f32[1792,32]{1,0:T(8,128)}), f32[224,32]{1,0:T(8,128)}) %reduce-scatter.4.cloned.1.call-update) | async-done | bytes 28688
  125.3 9.2 %all-gather.1 = f32[256,32]{1,0:T(8,128)S(1)} all-gather(f32[32,32]{1,0:T(8,128)S(1)} %fusion.16), channel_id=3, replica_groups=mesh['dp'=8,'expert'=4] {'dp'}, dimensions={0}, use_global_device_ids=true | all-gather | bytes 36864 | tf_op jit(solution)/shard_map/all_gather | solution.py:71
  134.6 2.9 %cholesky.16 = f32[32,32]{1,0:T(8,128)S(1)} custom-call(f32[32,32]{1,0:T(8,128)S(1)} %fusion.20), custom_call_target="Cholesky" | custom-call | tf_op jit(solution)/shard_map/jit(cholesky)/cholesky | solution.py:73
  138.9 2.4 %custom-call.7 = f32[1,32,32]{1,2,0:T(8,128)S(1)} custom-call(f32[1,32,32]{2,1,0:T(8,128)S(1)} %fusion.18), custom_call_target="InvertDiagBlocksLowerTriangular" | custom-call | tf_op jit(solution)/shard_map/jit(_solve_triangular)/triangular_solve | solution.py:74
  141.5 8.5 %all-gather.2 = f32[8,224,32]{1,2,0:T(8,128)S(1)} all-gather(f32[1,224,32]{1,2,0:T(8,128)S(1)} %convolution_bitcast_fusion.1), channel_id=1, replica_groups=mesh['dp'=8,'expert'=4] {'dp'}, dimensions={0}, use_global_device_ids=true | all-gather | bytes 258048 | tf_op jit(solution)/shard_map/all_gather | solution.py:75
  150.4 4.2 %convolution_convert_fusion.3 = bf16[32,512]{1,0:T(8,128)(2,1)S(1)} fusion(f32[1792,32]{0,1:T(8,128)S(1)} %reshape.138, f32[1792,512]{1,0:T(8,128)} %copy-done.1), kind=kOutput, calls=%fused_computation.14 | convolution fusion | flops 352337920 | bytes 3932160 | tf_op jit(solution)/shard_map/dot_general | solution.py:77
  154.6 23.6 %psum.7 = bf16[32,512]{1,0:T(8,128)(2,1)S(1)} all-reduce(bf16[32,512]{1,0:T(8,128)(2,1)S(1)} %convolution_convert_fusion.3), channel_id=1, replica_groups=mesh['dp'=8,'expert'=4] {'dp'}, use_global_device_ids=true, to_apply=%region_8.9 | all-reduce | flops 16384 | bytes 65536 | tf_op jit(solution)/shard_map/psum | solution.py:77
  178.2 3.1 %fusion.11 = f32[1792,512]{1,0:T(8,128)S(1)} fusion(f32[1792,32]{0,1:T(8,128)S(1)} %reshape.138, bf16[32,512]{1,0:T(8,128)(2,1)S(1)} %psum.7), kind=kOutput, calls=%fused_computation.24 | convolution fusion | flops 352354304 | bytes 3932160 | tf_op jit(solution)/shard_map/dot_general | solution.py:82
  182.1 2.0 %fusion = bf16[1,1,1792,512]{3,2,1,0:T(8,128)(2,1)} fusion(f32[1792,512]{1,0:T(8,128)S(1)} %copy-done.2, f32[1792,512]{1,0:T(8,128)S(1)} %fusion.11), kind=kLoop, calls=%fused_computation.6 | loop fusion | flops 1835008 | bytes 9175040 | tf_op jit(solution)/shard_map/broadcast_in_dim | solution.py:83
  184.1 1.3 gather_fusion
  185.8 4.5 %multiply_reduce_fusion = bf16[128,1792]{1,0:T(8,128)(2,1)} fusion(bf16[128,2,1792]{2,1,0:T(2,128)(2,1)S(1)} %gather.7, pred[128,2]{1,0:T(8,128)(4,1)S(1)} %copy.38, f32[128,2]{1,0:T(8,128)S(1)} %copy.39), kind=kLoop, calls=%fused_computation.10 | loop fusion | flops 1605632 | bytes 1377536 | tf_op jit(solution)/shard_map/reduce_sum | solution.py:65
  (59 shorter events, 12.0 us)
Async XLA Ops:
  7.2 77.6 %copy-start = (f32[1,512,32]{1,2,0:T(8,128)S(1)}, f32[1,512,32]{1,2,0:T(8,128)}, u32[]{:S(2)}) copy-start(f32[1,512,32]{1,2,0:T(8,128)} %param.13) | copy-start | bytes 196612
  7.2 12.0 %copy-start.4 = (bf16[128,1792]{1,0:T(8,128)(2,1)S(1)}, bf16[128,1792]{1,0:T(8,128)(2,1)}, u32[]{:S(2)}) copy-start(bf16[128,1792]{1,0:T(8,128)(2,1)} %param.7) | copy-start | bytes 1376260
  12.1 20.8 %all-to-all-start = ((bf16[4,128,512]{2,1,0:T(8,128)(2,1)}), bf16[4,128,512]{2,1,0:T(8,128)(2,1)S(1)}, u32[]{:S(2)}, u32[]{:S(2)}) async-start(bf16[4,128,512]{2,1,0:T(8,128)(2,1)} %bitcast.2), calls=%async_computation | async-start | bytes 1048576 | tf_op jit(solution)/shard_map/all_to_all | solution.py:41
  18.5 60.3 %all-gather.5.cloned.1.call-start = ((), (), s32[]{:S(2)}) async-start(), calls=%async_computation.4 | async-start | bytes 2064384 | tf_op jit(solution)/shard_map/all_gather | solution.py:47
  20.9 2.6 %copy-start.6 = (f32[128,2]{0,1:T(2,128)S(1)}, f32[128,2]{0,1:T(2,128)}, u32[]{:S(2)}) copy-start(f32[128,2]{0,1:T(2,128)} %param.9) | copy-start | bytes 3076
  33.0 3.9 %copy-start.5 = (s32[128,2]{0,1:T(2,128)S(1)}, s32[128,2]{0,1:T(2,128)}, u32[]{:S(2)}) copy-start(s32[128,2]{0,1:T(2,128)} %param.8) | copy-start | bytes 3076
  33.0 45.8 %all-to-all-start.1 = ((bf16[4,128,1792]{2,1,0:T(8,128)(2,1)}), bf16[4,128,1792]{2,1,0:T(8,128)(2,1)S(1)}, u32[]{:S(2)}, u32[]{:S(2)}) async-start(bf16[4,128,1792]{2,1,0:T(8,128)(2,1)} %bitcast.75), calls=%async_computation.1 | async-start | bytes 3670016 | tf_op jit(solution)/shard_map/all_to_all | solution.py:40
  36.7 87.5 %reduce-scatter.4.cloned.1.call-start = ((), (), s32[]{:S(2)}) async-start(), calls=%async_computation.5 | async-start | bytes 1032192
  78.8 3.0 %copy-start.3 = (bf16[1,1,1792,512]{3,2,1,0:T(8,128)(2,1)S(1)}, bf16[1,1,1792,512]{3,2,1,0:T(8,128)(2,1)}, u32[]{:S(2)}) copy-start(bf16[1,1,1792,512]{3,2,1,0:T(8,128)(2,1)} %param.12) | copy-start | bytes 5505028
  83.0 1.8 copy-start.1
  93.4 90.7 %all-to-all-start.2 = ((bf16[4,128,1792]{2,1,0:T(8,128)(2,1)}), bf16[4,128,1792]{2,1,0:T(8,128)(2,1)S(1)}, u32[]{:S(2)}, u32[]{:S(2)}) async-start(bf16[4,128,1792]{2,1,0:T(8,128)(2,1)} %bitcast.77), calls=%async_computation.2 | async-start | bytes 3670016 | tf_op jit(solution)/shard_map/all_to_all | solution.py:61
  178.2 3.9 %copy-start.2 = (f32[1792,512]{1,0:T(8,128)S(1)}, f32[1792,512]{1,0:T(8,128)}, u32[]{:S(2)}) copy-start(f32[1792,512]{1,0:T(8,128)} %copy-done.1) | copy-start | bytes 11010052
Sparse Core Ops, SparseCore 0:
  21.2 28.1 all-gather.4
  89.6 34.5 reduce-scatter.3
